TPU v7x, 32 devices: a whole 2x2x4 slice. The times are simulated.
32 devices in a mesh: seq: 8 (over z, y), head: 4 (over x, core).
Axes of the slice: x: 2, y: 2, z: 4, core: 2. Of those that a mesh axis runs over, the one named last changes fastest.
Arguments:
- query: bfloat16 [8, 40, 128], P(None, 'head'), may hold values from -400 to 400
- key_cache: bfloat16 [8, 4096, 8, 128], P(None, 'seq', 'head'), may hold values from -6 to 6
- value_cache: bfloat16 [8, 4096, 8, 128], P(None, 'seq', 'head'), may hold values from -6 to 6
- new_key: bfloat16 [8, 8, 128], P(None, 'head'), may hold values from -6 to 6
- new_value: bfloat16 [8, 8, 128], P(None, 'head'), may hold values from -6 to 6
- lengths: int32 [8], replicated, may hold values from 1024 to 4096, as said below
- out_weight: bfloat16 [5120, 5120], P('head', 'seq'), may hold values from -0.078125 to 0.078125
Outputs:
- projected: float32 [8, 5120], P(None, 'seq')
Inputs may be any that keep to these rules, and one draw needn't show every extreme that they name: `lengths`: some sequence has exactly 4096 cached tokens.
All inputs are finite; a program needn't handle non-finite values.
Results may differ from a plain program's by a relative error of at most 0.0064.
Values sent between devices are 32-bit elements; how exact they have to be, the bound alone decides.
A program may use at most 64 MiB of HBM per device.

v0:
```python
import math

import jax
import jax.numpy as jnp
from jax import lax
from jax.sharding import PartitionSpec as P

THETA_BASE = 10000000.0
NEG_FILL = -1e30


def apply_rotary(values, positions):
    half_width = values.shape[-1] // 2
    frequency = jnp.exp(
        jnp.arange(half_width, dtype=jnp.float32)
        * jnp.float32(-2.0 * math.log(THETA_BASE) / values.shape[-1])
    )
    angles = positions[..., None] * frequency
    cos_part = jnp.cos(angles)
    sin_part = jnp.sin(angles)
    lower_section = values[..., :half_width]
    upper_half = values[..., half_width:]
    return jnp.concatenate(
        [
            lower_section * cos_part - upper_half * sin_part,
            upper_half * cos_part + lower_section * sin_part,
        ],
        axis=-1,
    )


def query_positions(lengths, stretch_len):
    remainder = lengths % stretch_len
    return jnp.stack(
        [
            remainder,
            remainder + stretch_len,
            jnp.zeros_like(remainder) + (stretch_len + stretch_len // 2),
        ],
        axis=-1,
    ).astype(jnp.float32)


def body(query, key_cache, value_cache, new_key, new_value, lengths, out_weight):
    seq_count = lax.axis_size("seq")
    batch, span_len, kv_local, head_width = key_cache.shape
    heads_local = query.shape[1]
    group_size = heads_local // kv_local
    stretch_len = span_len * seq_count // 8
    scaling = 1.0 / math.sqrt(head_width)
    positions = lax.axis_index("seq") * span_len + jnp.arange(span_len, dtype=jnp.int32)
    query_pos = query_positions(lengths, stretch_len)
    query_rot = apply_rotary(query.astype(jnp.float32)[:, None], query_pos[:, :, None]).astype(
        jnp.bfloat16
    )
    key_rot = apply_rotary(
        key_cache.astype(jnp.float32), (positions % stretch_len).astype(jnp.float32)[None, :, None]
    ).astype(jnp.bfloat16)
    query_by_group = query_rot.reshape(batch, 3, kv_local, group_size, head_width)
    query_stretch = lengths // stretch_len
    key_stretch = positions // stretch_len
    key_class = jnp.where(
        key_stretch[None] == query_stretch[:, None],
        0,
        jnp.where(key_stretch[None] == query_stretch[:, None] - 1, 1, 2),
    )
    block_class = key_class[:, 0][:, None, None, None]
    picked = jnp.where(
        block_class == 0,
        query_by_group[:, 0],
        jnp.where(block_class == 1, query_by_group[:, 1], query_by_group[:, 2]),
    )
    selected_branch = (
        jnp.einsum("bkgd,bpkd->bkgp", picked, key_rot, preferred_element_type=jnp.float32) * scaling
    )
    live_mask = (positions[None] < lengths[:, None])[:, None, None, :]
    masked = jnp.where(live_mask, selected_branch, NEG_FILL)
    block_max = jnp.max(masked, axis=-1)
    weights = jnp.where(live_mask, jnp.exp(masked - block_max[..., None]), 0.0)
    block_total = jnp.sum(weights, axis=-1)
    block_acc = jnp.einsum(
        "bkgp,bpkd->bkgd",
        weights.astype(jnp.bfloat16),
        value_cache,
        preferred_element_type=jnp.float32,
    )
    current_key = apply_rotary(new_key.astype(jnp.float32), query_pos[:, 0][:, None]).astype(
        jnp.bfloat16
    )
    self_score = (
        jnp.einsum(
            "lmzu,lmu->lmz", query_by_group[:, 0], current_key, preferred_element_type=jnp.float32
        )
        * scaling
    )
    fresh_values = new_value.astype(jnp.float32)[:, :, None, :]
    top_score = lax.pmax(jnp.maximum(block_max, self_score), "seq")
    factor = jnp.exp(block_max - top_score)
    summed_total, summed_acc = lax.psum(
        (block_total * factor, block_acc * factor[..., None]), "seq"
    )
    self_factor = jnp.exp(self_score - top_score)
    total = summed_total + self_factor
    accum = summed_acc + fresh_values * self_factor[..., None]
    attended = (
        (accum / total[..., None]).reshape(batch, heads_local * head_width).astype(jnp.bfloat16)
    )
    partial_value = jnp.dot(attended, out_weight, preferred_element_type=jnp.float32)
    return lax.psum(partial_value, "head")


def solution(mesh):
    placed = (
        P(None, "head", None),
        P(None, "seq", "head", None),
        P(None, "seq", "head", None),
        P(None, "head", None),
        P(None, "head", None),
        P(),
        P("head", "seq"),
    )
    return jax.shard_map(
        body, mesh=mesh, in_specs=placed, out_specs=P(None, "seq"), check_vma=False
    )
```

profile of v0, /device:TPU:0, one launch (start us, length us, event | category | flops | bytes accessed | tf_op | source)
XLA Modules:
  0.0 84.6 jit_solution(15212608247679977557)
XLA Ops:
  0.0 4.1 %copy_convert_fusion = f32[8,512,2,128]{3,1,2,0:T(8,128)} fusion(bf16[8,512,2,128]{3,2,1,0:T(2,128)(2,1)} %param.8), kind=kLoop, calls=%fused_computation.8 | loop fusion | flops 1048576 | bytes 6291456 | tf_op jit(solution)/shard_map/convert_element_type | solution.py:57
  4.1 1.0 %multiply_cosine_fusion = (f32[512,64]{1,0:T(8,128)S(1)}, f32[512,64]{1,0:T(8,128)S(1)}) fusion(f32[64]{0:T(128)S(1)} %multiply_exponential_fusion, f32[512]{0:T(512)S(1)} %get-tuple-element.35), kind=kLoop, calls=%fused_computation.13 | loop fusion | flops 32768 | bytes 264448 | tf_op jit(solution)/shard_map/cos | solution.py:19
  5.1 0.0 copy-start.1
  5.1 4.9 %subtract_convert_fusion = (bf16[8,512,2,64]{3,1,2,0:T(8,128)(2,1)S(1)}, bf16[8,512,2,64]{3,1,2,0:T(8,128)(2,1)S(1)}) fusion(f32[8,512,2,128]{3,1,2,0:T(8,128)} %copy_convert_fusion, f32[512,64]{1,0:T(8,128)S(1)} %get-tuple-element.27, f32[512,64]{1,0:T(8,128)S(1)} %get-tuple-element.26), kind=kLoop, calls=%fused_computation.1 | loop fusion | flops 4194304 | bytes 6553600 | tf_op jit(solution)/shard_map/convert.3
  10.1 0.1 pad.8.clone
  10.2 0.1 add_convert_fusion.3
  10.3 0.1 multiply_cosine_fusion.1
  10.4 0.1 fusion.46
  10.5 0.1 add_convert_fusion.1
  10.6 0.5 slice.45
  11.1 0.7 compare_bitcast_fusion.1
  11.8 0.1 broadcast_compare_fusion
  11.9 1.4 %fusion.47 = (f32[8,2,5]{2,1,0:T(2,128)S(1)}, f32[8,2,5,512]{3,2,1,0:T(8,128)S(1)}) fusion(bf16[8,512,2,64]{3,1,2,0:T(8,128)(2,1)S(1)} %get-tuple-element.17, bf16[8,512,2,64]{3,1,2,0:T(8,128)(2,1)S(1)} %get-tuple-element.16, bf16[8,3,2,5,64]{4,3,2,0,1:T(8,128)(2,1)S(1)} %get-tuple-element.19, bf16[8,3,2,5,64]{4,3,2,0,1:T(8,128)(2,1)S(1)} %get-tuple-element.18, ...), kind=kOutput, calls=%fused_computation.83 | convolution fusion | flops 14946224 | bytes 2326864 | tf_op jit(solution)/shard_map/bkgd,bpkd->bkgp/dot_general | solution.py:74
  13.3 0.2 fusion.15
  13.5 0.1 multiply_cosine_fusion.2
  13.6 0.1 subtract_convert_fusion.2
  13.7 0.1 maximum_bitcast_fusion
  13.8 0.2 fusion.33
  14.0 23.4 %pmax.7 = f32[8,2,5]{2,1,0:T(2,128)S(1)} all-reduce(f32[8,2,5]{2,1,0:T(2,128)S(1)} %multiply_maximum_fusion), channel_id=1, replica_groups=mesh['seq'=8,'head'=4] {'seq'}, use_global_device_ids=true, to_apply=%region_1.2 | all-reduce | flops 80 | bytes 640 | tf_op jit(solution)/shard_map/pmax | solution.py:97
  37.5 0.4 fusion.12
  37.9 33.9 %all-reduce = (f32[8,2,5,128]{3,2,1,0:T(8,128)S(1)}, f32[8,2,5]{2,1,0:T(2,128)S(1)}) all-reduce(f32[8,2,5,128]{3,2,1,0:T(8,128)S(1)} %fusion.12, f32[8,2,5]{2,1,0:T(2,128)S(1)} %bitcast.58), channel_id=1, replica_groups=mesh['seq'=8,'head'=4] {'seq'}, use_global_device_ids=true, to_apply=%region_2.3 | all-reduce | flops 10320 | bytes 82560 | tf_op jit(solution)/shard_map/psum | solution.py:99
  71.9 0.1 divide_convert_fusion
  72.0 1.8 %fusion.48 = f32[8,640]{1,0:T(8,128)S(1)} fusion(bf16[8,1280]{1,0:T(8,128)(2,1)S(1)} %convert_element_type.44, bf16[1280,640]{1,0:T(8,128)(2,1)} %param.13), kind=kOutput, calls=%fused_computation.84 | convolution fusion | flops 13107200 | bytes 1679360 | tf_op jit(solution)/shard_map/dot_general | solution.py:108
  73.8 10.9 %psum.23 = f32[8,640]{1,0:T(8,128)} all-reduce(f32[8,640]{1,0:T(8,128)S(1)} %fusion.48), channel_id=1, replica_groups=mesh['seq'=8,'head'=4] {'head'}, use_global_device_ids=true, to_apply=%region_5.6 | all-reduce | flops 5120 | bytes 40960 | tf_op jit(solution)/shard_map/psum | solution.py:109
  (25 shorter events, 0.2 us)
Async XLA Ops:
  0.0 37.5 %copy-start = (bf16[8,512,2,128]{3,2,1,0:T(2,128)(2,1)S(1)}, bf16[8,512,2,128]{3,2,1,0:T(2,128)(2,1)}, u32[]{:S(2)}) copy-start(bf16[8,512,2,128]{3,2,1,0:T(2,128)(2,1)} %param.9) | copy-start | bytes 6291460
  5.1 5.0 %copy-start.4 = (s32[8]{0:T(128)S(1)}, s32[8]{0:T(128)}, u32[]{:S(2)}) copy-start(s32[8]{0:T(128)} %param.12) | copy-start | bytes 100
  5.1 5.3 %copy-start.1 = (bf16[8,10,128]{2,0,1:T(8,128)(2,1)S(1)}, bf16[8,10,128]{2,0,1:T(8,128)(2,1)}, u32[]{:S(2)}) copy-start(bf16[8,10,128]{2,0,1:T(8,128)(2,1)} %param.7) | copy-start | bytes 61444
  11.9 1.6 %copy-start.2 = (bf16[8,2,128]{2,1,0:T(2,128)(2,1)S(1)}, bf16[8,2,128]{2,1,0:T(2,128)(2,1)}, u32[]{:S(2)}) copy-start(bf16[8,2,128]{2,1,0:T(2,128)(2,1)} %param.10) | copy-start | bytes 12292
  13.3 58.6 %copy-start.3 = (bf16[8,2,128]{2,1,0:T(2,128)(2,1)S(1)}, bf16[8,2,128]{2,1,0:T(2,128)(2,1)}, u32[]{:S(2)}) copy-start(bf16[8,2,128]{2,1,0:T(2,128)(2,1)} %param.11) | copy-start | bytes 12292
where the time goes:
time: 84.9 us; the launch traced here: 84.6 us
  blocking collectives  68.2 us (80%)
  other arithmetic  11.7 us (14%)
  matrix products  3.78 us (4%)
    psum x1, blocking collectives, body(): lax.psum((block_total * factor, block_acc * factor[..., None]), 'seq')  33.9 us
    pmax x1, blocking collectives, body(): top_score = lax.pmax(jnp.maximum(block_max, self_score), 'seq')  23.4 us
    psum x1, blocking collectives, body(): return lax.psum(partial_value, 'head')  10.9 us
    another operation x3, other arithmetic  5.08 us
    convert_element_type x1, other arithmetic, body(): key_cache.astype(jnp.float32)  4.08 us
    dot_general x1, matrix products, body(): jnp.dot(attended, out_weight, preferred_element_type=jnp.float32)  1.75 us

commit v1 on v0

v1 whole, which is shorter than its diff:
```python
import functools
import math

import jax
import jax.numpy as jnp
from jax import lax
from jax.experimental import pallas as pl
from jax.experimental.pallas import tpu as pltpu
from jax.sharding import PartitionSpec as P

THETA_BASE = 10000000.0
NEG_FILL = -1e30
F32 = jnp.float32
BF16 = jnp.bfloat16
MESH = pl.DeviceIdType.MESH


def iota(shape, axis):
    return lax.broadcasted_iota(jnp.int32, shape, axis)


def rotate(x, cos, sin):
    return x * cos + pltpu.roll(x, x.shape[-1] // 2, x.ndim - 1) * sin


def kernel(
    seq_n, head_n, stretch,
    q_hbm, k_hbm, v_hbm, nk_hbm, nv_hbm, len_hbm, w_hbm,
    out_ref,
    q_in, kbuf, vbuf, nk_in, nv_in, lens, wbuf,
    cosv, sinv, cost, sint, q_pick, q_intra, nk_rot, nv_f32,
    send1, recv1, send2, recv2, recv3,
    in_sem, k_sem, v_sem, s1_sem, r1_sem, s2_sem, r2_sem, s3_sem, r3_sem,
):
    me = lax.axis_index("seq")
    mh = lax.axis_index("head")
    batch, rows2, hd = k_hbm.shape
    heads = q_hbm.shape[0]
    kv = nk_hbm.shape[0] // batch
    span = rows2 // kv
    group = heads // kv
    pad = send1.shape[1]
    half = hd // 2
    per_owner = seq_n // batch
    scaling = 1.0 / math.sqrt(hd)
    stat_row = heads
    stat_off = pad

    upper = me // (seq_n // 2)

    def far_first(k, n):
        return upper * k + (1 - upper) * (n - 1 - k)

    def copy_in(src, dst, sem):
        c = pltpu.make_async_copy(src, dst, sem)
        c.start()
        return c

    small = [
        copy_in(len_hbm, lens, in_sem.at[0]),
        copy_in(q_hbm, q_in, in_sem.at[1]),
        copy_in(nk_hbm, nk_in, in_sem.at[2]),
        copy_in(nv_hbm, nv_in, in_sem.at[3]),
    ]

    def k_copy(k):
        b = far_first(k, batch)
        return pltpu.make_async_copy(k_hbm.at[b], kbuf.at[k], k_sem.at[k])

    def v_copy(k):
        b = far_first(k, batch)
        return pltpu.make_async_copy(v_hbm.at[b], vbuf.at[k], v_sem.at[k])

    for k in range(batch):
        k_copy(k).start()
        v_copy(k).start()
    w_copy = copy_in(w_hbm, wbuf, in_sem.at[4])

    barrier = pltpu.get_barrier_semaphore()

    def greet(d, c):
        pl.semaphore_signal(
            barrier, inc=1, device_id=(lax.rem(me + d, seq_n), mh), device_id_type=MESH
        )
        return c

    lax.fori_loop(1, seq_n, greet, 0)
    for d in range(1, head_n):
        pl.semaphore_signal(
            barrier, inc=1, device_id=(me, lax.rem(mh + d, head_n)), device_id_type=MESH
        )

    def freq(shape):
        lane = iota(shape, len(shape) - 1)
        f = jnp.exp(
            (lane % half).astype(F32) * F32(-2.0 * math.log(THETA_BASE) / hd)
        )
        return f, jnp.where(lane < half, F32(-1.0), F32(1.0))

    tile = 8
    per_tile = tile // kv
    tiles = rows2 // tile
    start = lax.rem(me * span, stretch)
    f, sign = freq((tiles, hd))
    a = (start + iota((tiles, hd), 0) * per_tile).astype(F32) * f
    cosv[...] = jnp.cos(a)
    sinv[...] = jnp.sin(a) * sign
    f8, sign8 = freq((tile, hd))
    a8 = (iota((tile, hd), 0) // kv).astype(F32) * f8
    c0 = jnp.cos(a8)
    s0 = jnp.sin(a8) * sign8

    def fill(t, c):
        cv = cosv[pl.ds(t, 1), :]
        sv = sinv[pl.ds(t, 1), :]
        at = pl.ds(pl.multiple_of(t * tile, tile), tile)
        cost[at, :] = cv * c0 - sv * s0
        sint[at, :] = sv * c0 + cv * s0
        return c

    lax.fori_loop(0, tiles, fill, 0, unroll=8)

    for c in small:
        c.wait()
    row_b = iota((batch, hd), 0)
    lv = jnp.zeros((batch, hd), jnp.int32)
    for b in range(batch):
        lv = jnp.where(row_b == b, lens[b], lv)
    block_stretch = (me * span) // stretch
    rem = lax.rem(lv, stretch)
    qc = lax.div(lv, stretch)
    t_pick = jnp.where(
        qc == block_stretch,
        rem,
        jnp.where(qc - 1 == block_stretch, rem + stretch, stretch + stretch // 2),
    )
    fb, signb = freq((batch, hd))
    a_p = t_pick.astype(F32) * fb
    a_i = rem.astype(F32) * fb
    cp, sp = jnp.cos(a_p), jnp.sin(a_p) * signb
    ci, si = jnp.cos(a_i), jnp.sin(a_i) * signb
    for h in range(heads):
        x = q_in[h].astype(F32)
        q_pick[:, h, :] = rotate(x, cp, sp).astype(BF16).astype(F32)
        q_intra[:, h, :] = rotate(x, ci, si).astype(BF16).astype(F32)
    for h in range(heads, pad):
        q_pick[:, h, :] = jnp.zeros((batch, hd), F32)
        q_intra[:, h, :] = jnp.zeros((batch, hd), F32)
    row_n = iota((kv * batch, hd), 0)
    ln = jnp.zeros((kv * batch, hd), jnp.int32)
    for b in range(batch):
        ln = jnp.where(row_n // kv == b, lens[b], ln)
    fn, signn = freq((kv * batch, hd))
    a_n = lax.rem(ln, stretch).astype(F32) * fn
    nk_rot[...] = (
        rotate(nk_in[...].astype(F32), jnp.cos(a_n), jnp.sin(a_n) * signn).astype(BF16).astype(F32)
    )
    nv_f32[...] = nv_in[...].astype(F32)

    col = iota((pad, rows2), 1)
    fits = (col % kv) == (iota((pad, rows2), 0) // group)
    pos = me * span + col // kv
    prow = iota((pad, hd), 0)
    plane = iota((pad, hd), 1)
    diag = prow == plane
    diag2 = prow + stat_off == plane

    def send1_copy(k):
        b = far_first(k, batch)
        return pltpu.make_async_remote_copy(
            src_ref=send1.at[k],
            dst_ref=recv1.at[me],
            send_sem=s1_sem.at[k],
            recv_sem=r1_sem.at[me],
            device_id=(b * per_owner, mh),
            device_id_type=MESH,
        )

    chunk = min(256, rows2)

    def local_block(k):
        b = far_first(k, batch)
        k_copy(k).wait()
        q = q_pick[b].astype(BF16)
        parts = []
        for j in range(rows2 // chunk):
            at = pl.ds(j * chunk, chunk)
            kr = rotate(kbuf[k, at, :].astype(F32), cost[at, :], sint[at, :]).astype(BF16)
            parts.append(
                lax.dot_general(q, kr, (((1,), (1,)), ((), ())), preferred_element_type=F32)
            )
        s = jnp.concatenate(parts, axis=1) * scaling
        live = jnp.logical_and(fits, pos < lens[b])
        s = jnp.where(live, s, NEG_FILL)
        bmax = jnp.max(s, axis=1, keepdims=True)
        w = jnp.where(live, jnp.exp(s - bmax), 0.0)
        btot = jnp.sum(w, axis=1, keepdims=True)
        v_copy(k).wait()
        acc = jnp.dot(w.astype(BF16), vbuf[k], preferred_element_type=F32)
        stats = jnp.where(diag, bmax, jnp.where(diag2, btot, 0.0))
        stats = jnp.where(prow < heads, stats, 0.0)
        stats = jnp.sum(stats, axis=0, keepdims=True)
        return jnp.where(prow < heads, acc, jnp.where(prow == stat_row, stats, 0.0))

    for k in range(batch):
        payload = local_block(k)
        if k == 0:
            pl.semaphore_wait(barrier, seq_n - 1 + head_n - 1)
        mine = far_first(k, batch) * per_owner == me

        @pl.when(jnp.logical_not(mine))
        def _():
            send1[k] = payload
            send1_copy(k).start()

        @pl.when(mine)
        def _():
            recv1[me] = payload

    def send2_copy(d, slot):
        return pltpu.make_async_remote_copy(
            src_ref=send2,
            dst_ref=recv2.at[slot],
            send_sem=s2_sem.at[d],
            recv_sem=r2_sem.at[slot],
            device_id=(d, mh),
            device_id_type=MESH,
        )

    def over_peers(body):
        def step(j, c):
            d = far_first(j, seq_n)

            @pl.when(d != me)
            def _():
                body(d)

            return c

        lax.fori_loop(0, seq_n, step, 0, unroll=seq_n <= 8)

    def recv1_wait(d):
        pltpu.make_async_remote_copy(
            src_ref=recv1.at[d],
            dst_ref=recv1.at[d],
            send_sem=s1_sem.at[0],
            recv_sem=r1_sem.at[d],
            device_id=(d, mh),
            device_id_type=MESH,
        ).wait_recv()

    def combine():
        b = me // per_owner
        sc = jnp.sum(
            q_intra[b]
            * jnp.where(
                prow < group, nk_rot[pl.ds(b * kv, 1), :], nk_rot[pl.ds(b * kv + 1, 1), :]
            ),
            axis=1,
            keepdims=True,
        ) * scaling
        self_row = jnp.sum(jnp.where(diag, sc, 0.0), axis=0, keepdims=True)
        fresh = jnp.where(
            prow < group, nv_f32[pl.ds(b * kv, 1), :], nv_f32[pl.ds(b * kv + 1, 1), :]
        )
        over_peers(recv1_wait)
        st = recv1[:, stat_row, :]
        top = jnp.maximum(jnp.max(st, axis=0, keepdims=True), self_row)
        fac = jnp.exp(st - top)
        fac_self = jnp.exp(self_row - top)
        tot = pltpu.roll(st, hd - stat_off, 1)
        total = jnp.sum(tot * fac, axis=0, keepdims=True) + fac_self

        def column(r):
            return jnp.sum(jnp.where(diag, r, 0.0), axis=1, keepdims=True)

        acc = fresh * column(fac_self)
        for n in range(seq_n):
            acc = acc + recv1[n] * column(fac[n : n + 1, :])
        att = jnp.where(prow < heads, acc / column(jnp.where(plane[:1] < heads, total, 1.0)), 0.0)
        return att.astype(BF16).astype(F32), b

    def owner():
        att, b = combine()
        send2[...] = att
        over_peers(lambda d: send2_copy(d, b).start())
        recv2[b] = att

    if per_owner == 1:
        owner()
    else:
        pl.when(lax.rem(me, per_owner) == 0)(owner)

    def recv2_wait(b):
        pltpu.make_async_remote_copy(
            src_ref=send2,
            dst_ref=recv2.at[b],
            send_sem=s2_sem.at[0],
            recv_sem=r2_sem.at[b],
            device_id=(b * per_owner, mh),
            device_id_type=MESH,
        ).wait_recv()

    w_copy.wait()
    for k in range(batch):
        b = far_first(k, batch)

        @pl.when(b * per_owner != me)
        def _():
            recv2_wait(b)

    att = jnp.concatenate([recv2[:, h, :] for h in range(heads)], axis=1).astype(BF16)
    partial = jnp.dot(att, wbuf[...], preferred_element_type=F32)
    recv3[mh] = partial

    def send3_copy(d):
        return pltpu.make_async_remote_copy(
            src_ref=recv3.at[mh],
            dst_ref=recv3.at[mh],
            send_sem=s3_sem.at[d],
            recv_sem=r3_sem.at[mh],
            device_id=(me, lax.rem(mh + d, head_n)),
            device_id_type=MESH,
        )

    for d in range(1, head_n):
        send3_copy(d).start()
    for d in range(1, head_n):
        src = lax.rem(mh + d, head_n)
        pltpu.make_async_remote_copy(
            src_ref=recv3.at[src],
            dst_ref=recv3.at[src],
            send_sem=s3_sem.at[d],
            recv_sem=r3_sem.at[src],
            device_id=(me, src),
            device_id_type=MESH,
        ).wait_recv()
    total = recv3[0]
    for h in range(1, head_n):
        total = total + recv3[h]
    out_ref[...] = total

    for k in range(batch):

        @pl.when(far_first(k, batch) * per_owner != me)
        def _():
            send1_copy(k).wait_send()

    def sends2():
        over_peers(lambda d: send2_copy(d, me // per_owner).wait_send())

    if per_owner == 1:
        sends2()
    else:
        pl.when(lax.rem(me, per_owner) == 0)(sends2)
    for d in range(1, head_n):
        send3_copy(d).wait_send()


def body(query, key_cache, value_cache, new_key, new_value, lengths, out_weight):
    seq_n = lax.axis_size("seq")
    head_n = lax.axis_size("head")
    batch, span, kv, hd = key_cache.shape
    heads = query.shape[1]
    cols = out_weight.shape[1]
    stretch = span * seq_n // 8
    pad = -(-(heads + 1) // 8) * 8
    rows2 = span * kv
    dma = pltpu.SemaphoreType.DMA
    hbm = pl.BlockSpec(memory_space=pltpu.HBM)
    return pl.pallas_call(
        functools.partial(kernel, seq_n, head_n, stretch),
        out_shape=jax.ShapeDtypeStruct((batch, cols), F32),
        in_specs=[hbm] * 7,
        out_specs=pl.BlockSpec(memory_space=pltpu.VMEM),
        scratch_shapes=[
            pltpu.VMEM((heads, batch, hd), BF16),
            pltpu.VMEM((batch, rows2, hd), BF16),
            pltpu.VMEM((batch, rows2, hd), BF16),
            pltpu.VMEM((batch * kv, hd), BF16),
            pltpu.VMEM((batch * kv, hd), BF16),
            pltpu.SMEM((batch,), jnp.int32),
            pltpu.VMEM(out_weight.shape, BF16),
            pltpu.VMEM((rows2 // 8, hd), F32),
            pltpu.VMEM((rows2 // 8, hd), F32),
            pltpu.VMEM((rows2, hd), F32),
            pltpu.VMEM((rows2, hd), F32),
            pltpu.VMEM((batch, pad, hd), F32),
            pltpu.VMEM((batch, pad, hd), F32),
            pltpu.VMEM((batch * kv, hd), F32),
            pltpu.VMEM((batch * kv, hd), F32),
            pltpu.VMEM((batch, pad, hd), F32),
            pltpu.VMEM((seq_n, pad, hd), F32),
            pltpu.VMEM((pad, hd), F32),
            pltpu.VMEM((batch, pad, hd), F32),
            pltpu.VMEM((head_n, batch, cols), F32),
            dma((5,)),
            dma((batch,)),
            dma((batch,)),
            dma((batch,)),
            dma((seq_n,)),
            dma((seq_n,)),
            dma((batch,)),
            dma((head_n,)),
            dma((head_n,)),
        ],
        compiler_params=pltpu.CompilerParams(collective_id=0, has_side_effects=True),
    )(
        jnp.transpose(query, (1, 0, 2)),
        key_cache.reshape(batch, rows2, hd),
        value_cache.reshape(batch, rows2, hd),
        new_key.reshape(batch * kv, hd),
        new_value.reshape(batch * kv, hd),
        lengths,
        out_weight,
    )


def solution(mesh):
    placed = (
        P(None, "head", None),
        P(None, "seq", "head", None),
        P(None, "seq", "head", None),
        P(None, "head", None),
        P(None, "head", None),
        P(),
        P("head", "seq"),
    )
    return jax.shard_map(
        body, mesh=mesh, in_specs=placed, out_specs=P(None, "seq"), check_vma=False
    )
```

time: 84.9 us -> 22.9 us (0.27)
  blocking collectives: 68.2 us -> 0 us
  Pallas kernels: 0 us -> 21.4 us
  other arithmetic: 11.7 us -> 0 us
  matrix products: 3.78 us -> 0 us
    psum x2 -> x0, blocking collectives: 44.8 us -> none  [the longest x1 33.9 us: body(): lax.psum((block_total * factor, block_acc * factor[..., None]), 'seq')]
    pmax x1 -> x0, blocking collectives: 23.4 us -> none  [body(): top_score = lax.pmax(jnp.maximum(block_max, self_score), 'seq')]
    pallas_call x0 -> x1, Pallas kernels: none -> 21.4 us  [body(): pl.pallas_call(functools.partial(kernel, seq_n, head_n, stretch), out_sha...]
    another operation x4 -> x0, other arithmetic: 5.09 us -> none
    convert_element_type x5 -> x0, other arithmetic: 4.26 us -> none  [the longest x1 4.08 us: body(): key_cache.astype(jnp.float32)]
    dot_general x4 -> x0, matrix products: 3.78 us -> none  [the longest x1 1.75 us: body(): jnp.dot(attended, out_weight, preferred_element_type=jnp.float32)]
    unnamed x10 -> x1, local copies, waits for them, and re-layouts: 0.02 us -> 1.34 us
    cos x3 -> x0, other arithmetic: 1.22 us -> none  [apply_rotary(): cos_part = jnp.cos(angles)]
where the time goes in v1:
time: 22.9 us; the launch traced here: 22.8 us
  Pallas kernels  21.4 us (93%)
  local copies, waits for them, and re-layouts  1.34 us (6%)
    pallas_call x1, Pallas kernels, body(): pl.pallas_call(functools.partial(kernel, seq_n, head_n, stretch), out_sha...  21.4 us
    unnamed x1, local copies, waits for them, and re-layouts  1.34 us

profile of v1, /device:TPU:0, one launch (start us, length us, event | category | flops | bytes accessed | tf_op | source)
XLA Modules:
  0.0 22.8 jit_solution(362855135303170533)
XLA Ops:
  0.0 21.4 %shard_map.73 = f32[8,640]{1,0:T(8,128)} custom-call(bf16[10,8,128]{2,1,0:T(8,128)(2,1)} %bitcast.7, bf16[8,1024,128]{2,1,0:T(8,128)(2,1)} %bitcast.5, bf16[8,1024,128]{2,1,0:T(8,128)(2,1)} %bitcast.6, bf16[16,128]{1,0:T(8,128)(2,1)} %bitcast.8, bf16[16,128]{1,0:T(8,128)(2,1)} %bitcast.9, s32[8]{0:T(128)} %len_hbm.1, bf16[1280,640]{1,0:T(8,128)(2,1)} %w_hbm.1), custom_call_target="tpu_custom_call" | custom-call | tf_op jit(solution)/shard_map/pallas_call | solution.py:371
  21.4 1.3 %copy.9 = f32[8,640]{1,0:T(8,128)} copy(f32[8,640]{1,0:T(8,128)} %shard_map.73) | data formatting | bytes 40960

commit v2 on v1

--- a/solution.py
+++ b/solution.py
@@ -39,17 +39,17 @@
     kv = nk_hbm.shape[0] // batch
     span = rows2 // kv
     group = heads // kv
-    pad = send1.shape[1]
+    pad = q_pick.shape[1]
     half = hd // 2
     per_owner = seq_n // batch
     scaling = 1.0 / math.sqrt(hd)
     stat_row = heads
     stat_off = pad
 
-    upper = me // (seq_n // 2)
-
-    def far_first(k, n):
-        return upper * k + (1 - upper) * (n - 1 - k)
+    away = sorted(range(1, batch), key=lambda d: -min(d, batch - d)) + [0]
+
+    def turn(k):
+        return lax.rem(me // per_owner + away[k], batch)
 
     def copy_in(src, dst, sem):
         c = pltpu.make_async_copy(src, dst, sem)
@@ -64,11 +64,11 @@
     ]
 
     def k_copy(k):
-        b = far_first(k, batch)
+        b = turn(k)
         return pltpu.make_async_copy(k_hbm.at[b], kbuf.at[k], k_sem.at[k])
 
     def v_copy(k):
-        b = far_first(k, batch)
+        b = turn(k)
         return pltpu.make_async_copy(v_hbm.at[b], vbuf.at[k], v_sem.at[k])
 
     for k in range(batch):
@@ -166,7 +166,7 @@
     diag2 = prow + stat_off == plane
 
     def send1_copy(k):
-        b = far_first(k, batch)
+        b = turn(k)
         return pltpu.make_async_remote_copy(
             src_ref=send1.at[k],
             dst_ref=recv1.at[me],
@@ -178,44 +178,50 @@
 
     chunk = min(256, rows2)
 
-    def local_block(k):
-        b = far_first(k, batch)
-        k_copy(k).wait()
-        q = q_pick[b].astype(BF16)
-        parts = []
-        for j in range(rows2 // chunk):
-            at = pl.ds(j * chunk, chunk)
-            kr = rotate(kbuf[k, at, :].astype(F32), cost[at, :], sint[at, :]).astype(BF16)
-            parts.append(
-                lax.dot_general(q, kr, (((1,), (1,)), ((), ())), preferred_element_type=F32)
-            )
-        s = jnp.concatenate(parts, axis=1) * scaling
-        live = jnp.logical_and(fits, pos < lens[b])
-        s = jnp.where(live, s, NEG_FILL)
-        bmax = jnp.max(s, axis=1, keepdims=True)
-        w = jnp.where(live, jnp.exp(s - bmax), 0.0)
-        btot = jnp.sum(w, axis=1, keepdims=True)
-        v_copy(k).wait()
-        acc = jnp.dot(w.astype(BF16), vbuf[k], preferred_element_type=F32)
-        stats = jnp.where(diag, bmax, jnp.where(diag2, btot, 0.0))
-        stats = jnp.where(prow < heads, stats, 0.0)
-        stats = jnp.sum(stats, axis=0, keepdims=True)
-        return jnp.where(prow < heads, acc, jnp.where(prow == stat_row, stats, 0.0))
-
-    for k in range(batch):
-        payload = local_block(k)
-        if k == 0:
-            pl.semaphore_wait(barrier, seq_n - 1 + head_n - 1)
-        mine = far_first(k, batch) * per_owner == me
-
-        @pl.when(jnp.logical_not(mine))
+    def local_blocks(ks):
+        scores = []
+        for k in ks:
+            k_copy(k).wait()
+            q = q_pick[turn(k)].astype(BF16)
+            parts = []
+            for j in range(rows2 // chunk):
+                at = pl.ds(j * chunk, chunk)
+                kr = rotate(kbuf[k, at, :].astype(F32), cost[at, :], sint[at, :]).astype(BF16)
+                parts.append(
+                    lax.dot_general(q, kr, (((1,), (1,)), ((), ())), preferred_element_type=F32)
+                )
+            scores.append(jnp.concatenate(parts, axis=1) * scaling)
+        for k, s in zip(ks, scores):
+            live = jnp.logical_and(fits, pos < lens[turn(k)])
+            s = jnp.where(live, s, NEG_FILL)
+            bmax = jnp.max(s, axis=1, keepdims=True)
+            w = jnp.where(live, jnp.exp(s - bmax), 0.0)
+            btot = jnp.sum(w, axis=1, keepdims=True)
+            v_copy(k).wait()
+            acc = jnp.dot(w.astype(BF16), vbuf[k], preferred_element_type=F32)
+            stats = jnp.where(diag, bmax, jnp.where(diag2, btot, 0.0))
+            stats = jnp.where(prow < heads, stats, 0.0)
+            stats = jnp.sum(stats, axis=0, keepdims=True)
+            send1[k] = jnp.where(prow < heads, acc, stats)[: heads + 1]
+
+    together = 2
+    for k in range(0, batch, together):
+        local_blocks(range(k, min(k + together, batch)))
+    pl.semaphore_wait(barrier, seq_n - 1 + head_n - 1)
+    for k in range(batch - 1):
+        send1_copy(k).start()
+    if per_owner == 1:
+        recv1[me] = send1[batch - 1]
+    else:
+        leads = lax.rem(me, per_owner) == 0
+
+        @pl.when(jnp.logical_not(leads))
         def _():
-            send1[k] = payload
-            send1_copy(k).start()
-
-        @pl.when(mine)
+            send1_copy(batch - 1).start()
+
+        @pl.when(leads)
         def _():
-            recv1[me] = payload
+            recv1[me] = send1[batch - 1]
 
     def send2_copy(d, slot):
         return pltpu.make_async_remote_copy(
@@ -227,17 +233,19 @@
             device_id_type=MESH,
         )
 
+    reach = sorted(range(1, seq_n), key=lambda d: -min(d, seq_n - d))
+
     def over_peers(body):
-        def step(j, c):
-            d = far_first(j, seq_n)
-
-            @pl.when(d != me)
-            def _():
-                body(d)
-
-            return c
-
-        lax.fori_loop(0, seq_n, step, 0, unroll=seq_n <= 8)
+        if seq_n <= 8:
+            for d in reach:
+                body(lax.rem(me + d, seq_n))
+        else:
+
+            def step(d, c):
+                body(lax.rem(me + d, seq_n))
+                return c
+
+            lax.fori_loop(1, seq_n, step, 0)
 
     def recv1_wait(d):
         pltpu.make_async_remote_copy(
@@ -272,12 +280,12 @@
         total = jnp.sum(tot * fac, axis=0, keepdims=True) + fac_self
 
         def column(r):
-            return jnp.sum(jnp.where(diag, r, 0.0), axis=1, keepdims=True)
-
-        acc = fresh * column(fac_self)
+            return jnp.sum(jnp.where(diag[:heads], r, 0.0), axis=1, keepdims=True)
+
+        acc = fresh[:heads] * column(fac_self)
         for n in range(seq_n):
-            acc = acc + recv1[n] * column(fac[n : n + 1, :])
-        att = jnp.where(prow < heads, acc / column(jnp.where(plane[:1] < heads, total, 1.0)), 0.0)
+            acc = acc + recv1[n, :heads, :] * column(fac[n : n + 1, :])
+        att = acc / column(total)
         return att.astype(BF16).astype(F32), b
 
     def owner():
@@ -289,7 +297,7 @@
     if per_owner == 1:
         owner()
     else:
-        pl.when(lax.rem(me, per_owner) == 0)(owner)
+        pl.when(leads)(owner)
 
     def recv2_wait(b):
         pltpu.make_async_remote_copy(
@@ -302,12 +310,13 @@
         ).wait_recv()
 
     w_copy.wait()
-    for k in range(batch):
-        b = far_first(k, batch)
-
-        @pl.when(b * per_owner != me)
+    for k in range(batch - 1):
+        recv2_wait(turn(k))
+    if per_owner > 1:
+
+        @pl.when(jnp.logical_not(leads))
         def _():
-            recv2_wait(b)
+            recv2_wait(turn(batch - 1))
 
     att = jnp.concatenate([recv2[:, h, :] for h in range(heads)], axis=1).astype(BF16)
     partial = jnp.dot(att, wbuf[...], preferred_element_type=F32)
@@ -335,16 +344,15 @@
             device_id=(me, src),
             device_id_type=MESH,
         ).wait_recv()
-    total = recv3[0]
-    for h in range(1, head_n):
-        total = total + recv3[h]
-    out_ref[...] = total
-
-    for k in range(batch):
-
-        @pl.when(far_first(k, batch) * per_owner != me)
+    out_ref[...] = recv3[...]
+
+    for k in range(batch - 1):
+        send1_copy(k).wait_send()
+    if per_owner > 1:
+
+        @pl.when(jnp.logical_not(leads))
         def _():
-            send1_copy(k).wait_send()
+            send1_copy(batch - 1).wait_send()
 
     def sends2():
         over_peers(lambda d: send2_copy(d, me // per_owner).wait_send())
@@ -352,7 +360,7 @@
     if per_owner == 1:
         sends2()
     else:
-        pl.when(lax.rem(me, per_owner) == 0)(sends2)
+        pl.when(leads)(sends2)
     for d in range(1, head_n):
         send3_copy(d).wait_send()
 
@@ -368,9 +376,9 @@
     rows2 = span * kv
     dma = pltpu.SemaphoreType.DMA
     hbm = pl.BlockSpec(memory_space=pltpu.HBM)
-    return pl.pallas_call(
+    res = pl.pallas_call(
         functools.partial(kernel, seq_n, head_n, stretch),
-        out_shape=jax.ShapeDtypeStruct((batch, cols), F32),
+        out_shape=pltpu.VMEM((head_n, batch, cols), F32),
         in_specs=[hbm] * 7,
         out_specs=pl.BlockSpec(memory_space=pltpu.VMEM),
         scratch_shapes=[
@@ -389,10 +397,10 @@
             pltpu.VMEM((batch, pad, hd), F32),
             pltpu.VMEM((batch * kv, hd), F32),
             pltpu.VMEM((batch * kv, hd), F32),
-            pltpu.VMEM((batch, pad, hd), F32),
-            pltpu.VMEM((seq_n, pad, hd), F32),
-            pltpu.VMEM((pad, hd), F32),
-            pltpu.VMEM((batch, pad, hd), F32),
+            pltpu.VMEM((batch, heads + 1, hd), F32),
+            pltpu.VMEM((seq_n, heads + 1, hd), F32),
+            pltpu.VMEM((heads, hd), F32),
+            pltpu.VMEM((batch, heads, hd), F32),
             pltpu.VMEM((head_n, batch, cols), F32),
             dma((5,)),
             dma((batch,)),
@@ -414,6 +422,7 @@
         lengths,
         out_weight,
     )
+    return jnp.sum(res, axis=0)
 
 
 def solution(mesh):

time: 22.9 us -> 20.7 us (0.904)
  Pallas kernels: 21.4 us -> 19.9 us
  local copies, waits for them, and re-layouts: 1.34 us -> 0 us
  other arithmetic: 0 us -> 0.61 us
    pallas_call x1, Pallas kernels: 21.4 us -> 19.9 us  [body(): pl.pallas_call(functools.partial(kernel, seq_n, head_n, stretch), out_sha...]
    unnamed x1 -> x0, local copies, waits for them, and re-layouts: 1.34 us -> none
    reduce_sum x0 -> x1, other arithmetic: none -> 0.61 us  [body(): return jnp.sum(res, axis=0)]
where the time goes in v2:
time: 20.7 us; the launch traced here: 20.5 us
  Pallas kernels  19.9 us (96%)
  other arithmetic  0.61 us (3%)
    pallas_call x1, Pallas kernels, body(): pl.pallas_call(functools.partial(kernel, seq_n, head_n, stretch), out_sha...  19.9 us
    reduce_sum x1, other arithmetic, body(): return jnp.sum(res, axis=0)  0.61 us

profile of v2, /device:TPU:0, one launch (start us, length us, event | category | flops | bytes accessed | tf_op | source)
XLA Modules:
  0.0 20.5 jit_solution(8182030472454080761)
XLA Ops:
  0.0 19.9 %shard_map.73 = f32[4,8,640]{2,1,0:T(8,128)S(1)} custom-call(bf16[10,8,128]{2,1,0:T(8,128)(2,1)} %bitcast.7, bf16[8,1024,128]{2,1,0:T(8,128)(2,1)} %bitcast.5, bf16[8,1024,128]{2,1,0:T(8,128)(2,1)} %bitcast.6, bf16[16,128]{1,0:T(8,128)(2,1)} %bitcast.8, bf16[16,128]{1,0:T(8,128)(2,1)} %bitcast.9, s32[8]{0:T(128)} %len_hbm.1, bf16[1280,640]{1,0:T(8,128)(2,1)} %w_hbm.1), custom_call_target="tpu_custom_call" | custom-call | tf_op jit(solution)/shard_map/pallas_call | solution.py:379
  19.9 0.6 %reduce_sum.9 = f32[8,640]{1,0:T(8,128)} reduce(f32[4,8,640]{2,1,0:T(8,128)S(1)} %shard_map.73, f32[]{:T(128)} %constant.0.clone.1), dimensions={0}, to_apply=%region_0.0 | reduce | flops 15360 | bytes 102404 | tf_op jit(solution)/shard_map/reduce_sum | solution.py:425

commit v3 on v2

--- a/solution.py
+++ b/solution.py
@@ -101,10 +101,18 @@
     per_tile = tile // kv
     tiles = rows2 // tile
     start = lax.rem(me * span, stretch)
-    f, sign = freq((tiles, hd))
-    a = (start + iota((tiles, hd), 0) * per_tile).astype(F32) * f
-    cosv[...] = jnp.cos(a)
-    sinv[...] = jnp.sin(a) * sign
+    fine = min(16, tiles)
+    coarse = tiles // fine
+    ff, signf = freq((fine, hd))
+    af = (iota((fine, hd), 0) * per_tile).astype(F32) * ff
+    cf, sf = jnp.cos(af), jnp.sin(af)
+    fc, _ = freq((coarse, hd))
+    ac = (start + iota((coarse, hd), 0) * (fine * per_tile)).astype(F32) * fc
+    cc, sc = jnp.cos(ac), jnp.sin(ac)
+    for j in range(coarse):
+        cr, sr = cc[j : j + 1], sc[j : j + 1]
+        cosv[j * fine : (j + 1) * fine] = cr * cf - sr * sf
+        sinv[j * fine : (j + 1) * fine] = (sr * cf + cr * sf) * signf
     f8, sign8 = freq((tile, hd))
     a8 = (iota((tile, hd), 0) // kv).astype(F32) * f8
     c0 = jnp.cos(a8)
@@ -205,10 +213,14 @@
             send1[k] = jnp.where(prow < heads, acc, stats)[: heads + 1]
 
     together = 2
+    early = batch - together
     for k in range(0, batch, together):
         local_blocks(range(k, min(k + together, batch)))
-    pl.semaphore_wait(barrier, seq_n - 1 + head_n - 1)
-    for k in range(batch - 1):
+        if k + together == early:
+            pl.semaphore_wait(barrier, seq_n - 1 + head_n - 1)
+            for j in range(early):
+                send1_copy(j).start()
+    for k in range(early, batch - 1):
         send1_copy(k).start()
     if per_owner == 1:
         recv1[me] = send1[batch - 1]

time: 20.7 us -> 20.4 us (0.986)
    pallas_call x1, Pallas kernels: 19.9 us -> 19.7 us  [body(): pl.pallas_call(functools.partial(kernel, seq_n, head_n, stretch), out_sha...]
where the time goes in v3:
time: 20.4 us; the launch traced here: 20.3 us
  Pallas kernels  19.7 us (97%)
  other arithmetic  0.61 us (3%)
    pallas_call x1, Pallas kernels, body(): pl.pallas_call(functools.partial(kernel, seq_n, head_n, stretch), out_sha...  19.7 us
    reduce_sum x1, other arithmetic, body(): return jnp.sum(res, axis=0)  0.61 us

profile of v3, /device:TPU:0, one launch (start us, length us, event | category | flops | bytes accessed | tf_op | source)
XLA Modules:
  0.0 20.3 jit_solution(10618100674864880357)
XLA Ops:
  0.0 19.7 %shard_map.73 = f32[4,8,640]{2,1,0:T(8,128)S(1)} custom-call(bf16[10,8,128]{2,1,0:T(8,128)(2,1)} %bitcast.7, bf16[8,1024,128]{2,1,0:T(8,128)(2,1)} %bitcast.5, bf16[8,1024,128]{2,1,0:T(8,128)(2,1)} %bitcast.6, bf16[16,128]{1,0:T(8,128)(2,1)} %bitcast.8, bf16[16,128]{1,0:T(8,128)(2,1)} %bitcast.9, s32[8]{0:T(128)} %len_hbm.1, bf16[1280,640]{1,0:T(8,128)(2,1)} %w_hbm.1), custom_call_target="tpu_custom_call" | custom-call | tf_op jit(solution)/shard_map/pallas_call | solution.py:391
  19.7 0.6 %reduce_sum.9 = f32[8,640]{1,0:T(8,128)} reduce(f32[4,8,640]{2,1,0:T(8,128)S(1)} %shard_map.73, f32[]{:T(128)} %constant.0.clone.1), dimensions={0}, to_apply=%region_0.0 | reduce | flops 15360 | bytes 102404 | tf_op jit(solution)/shard_map/reduce_sum | solution.py:437

commit v4 on v3

--- a/solution.py
+++ b/solution.py
@@ -194,7 +194,9 @@
             parts = []
             for j in range(rows2 // chunk):
                 at = pl.ds(j * chunk, chunk)
-                kr = rotate(kbuf[k, at, :].astype(F32), cost[at, :], sint[at, :]).astype(BF16)
+                raw = kbuf[k, at, :]
+                turned = pltpu.roll(raw, hd // 2, 1).astype(F32)
+                kr = (raw.astype(F32) * cost[at, :] + turned * sint[at, :]).astype(BF16)
                 parts.append(
                     lax.dot_general(q, kr, (((1,), (1,)), ((), ())), preferred_element_type=F32)
                 )

time: 20.4 us -> 20.4 us (level)
  no operation moved by 1% of the time
where the time goes in v4:
time: 20.4 us; the launch traced here: 20.2 us
  Pallas kernels  19.6 us (96%)
  other arithmetic  0.61 us (3%)
    pallas_call x1, Pallas kernels, body(): pl.pallas_call(functools.partial(kernel, seq_n, head_n, stretch), out_sha...  19.6 us
    reduce_sum x1, other arithmetic, body(): return jnp.sum(res, axis=0)  0.61 us

profile of v4, /device:TPU:0, one launch (start us, length us, event | category | flops | bytes accessed | tf_op | source)
XLA Modules:
  0.0 20.2 jit_solution(13232345088399289137)
XLA Ops:
  0.0 19.6 %shard_map.73 = f32[4,8,640]{2,1,0:T(8,128)S(1)} custom-call(bf16[10,8,128]{2,1,0:T(8,128)(2,1)} %bitcast.7, bf16[8,1024,128]{2,1,0:T(8,128)(2,1)} %bitcast.5, bf16[8,1024,128]{2,1,0:T(8,128)(2,1)} %bitcast.6, bf16[16,128]{1,0:T(8,128)(2,1)} %bitcast.8, bf16[16,128]{1,0:T(8,128)(2,1)} %bitcast.9, s32[8]{0:T(128)} %len_hbm.1, bf16[1280,640]{1,0:T(8,128)(2,1)} %w_hbm.1), custom_call_target="tpu_custom_call" | custom-call | tf_op jit(solution)/shard_map/pallas_call | solution.py:393
  19.6 0.6 %reduce_sum.9 = f32[8,640]{1,0:T(8,128)} reduce(f32[4,8,640]{2,1,0:T(8,128)S(1)} %shard_map.73, f32[]{:T(128)} %constant.0.clone.1), dimensions={0}, to_apply=%region_0.0 | reduce | flops 15360 | bytes 102404 | tf_op jit(solution)/shard_map/reduce_sum | solution.py:439
